TPU v7x, 32 devices: a whole 2x2x4 slice. The times are simulated.
32 devices in a mesh: dp: 8 (over z, y), mp: 4 (over x, core).
Axes of the slice: x: 2, y: 2, z: 4, core: 2. Of those that a mesh axis runs over, the one named last changes fastest.
Arguments:
- tokens: bfloat16 [8, 1024, 1280], P('dp', 'mp'), may hold values from -6 to 6
- sizes: float32 [8, 1024], P('dp'), may hold values from 1 to 8
- ln1_gain: float32 [1280], replicated, may hold values from 0.25 to 1.75
- qkv_weight: bfloat16 [3, 1280, 1280], P(None, 'dp', 'mp'), may hold values from -0.15625 to 0.15625
- proj_weight: bfloat16 [1280, 1280], P('mp', 'dp'), may hold values from -0.15625 to 0.15625
- ln2_gain: float32 [1280], replicated, may hold values from 0.25 to 1.75
- fc1_weight: bfloat16 [1280, 5120], P('dp', 'mp'), may hold values from -0.15625 to 0.15625
- fc1_bias: float32 [5120], P('mp'), may hold values from -3 to 3
- fc2_weight: bfloat16 [5120, 1280], P('mp', 'dp'), may hold values from -0.078125 to 0.078125
- pair_source: int32 [8, 16], P('dp'), may hold values from 0 to 1022, as said below
- pair_target: int32 [8, 16], P('dp'), may hold values from 1 to 1023, as said below
- kept_order: int32 [8, 1008], P('dp'), may hold values from 0 to 1023, as said below
Outputs:
- merged_out: bfloat16 [8, 1008, 1280], P('dp', 'mp')
Inputs may be any that keep to these rules, and one draw needn't show every extreme that they name: `pair_source`: in each image the 16 entries are distinct even token indices. `pair_target`: odd token indices; several sources may join the same target. `kept_order`: in each image every token index that is not in pair_source appears exactly once.
All inputs are finite; a program needn't handle non-finite values.
Results may differ from a plain program's by a relative error of at most 0.017.
Values may be sent and summed in bfloat16 or wider, within the bound.
A program may use at most 64 MiB of HBM per device.

v0:
```python
import math
import jax
import jax.numpy as jnp
from jax import lax
from jax.sharding import PartitionSpec as P

D = 1280
HEADS = 16


def layer_norm(values, gain):
    center = values - jnp.mean(values, axis=-1, keepdims=True)
    spread = jnp.mean(center * center, axis=-1, keepdims=True)
    return center * lax.rsqrt(spread + 1e-06) * gain


def merge_rows(total, order_rows, source_ids, target_ids):
    kept_rows = jnp.take_along_axis(total, order_rows[:, :, None], axis=1)
    source_rows = jnp.take_along_axis(total, source_ids[:, :, None], axis=1)
    joins = (order_rows[:, :, None] == target_ids[:, None, :]).astype(jnp.float32)
    return kept_rows + jnp.einsum(
        "icr,ird->icd", joins, source_rows, precision=lax.Precision.HIGHEST
    )


def shards(
    tokens,
    sizes,
    ln1_gain,
    qkv_weight,
    proj_weight,
    ln2_gain,
    fc1_weight,
    fc1_bias,
    fc2_weight,
    pair_source,
    pair_target,
    kept_order,
):
    images, own_tokens, width = tokens.shape
    length = sizes.shape[1]
    kept_total = kept_order.shape[1]
    devices_mp = lax.axis_size("mp")
    own_start = lax.axis_index("mp") * own_tokens
    head_size = D // HEADS
    base = tokens.astype(jnp.float32)
    normed = layer_norm(base, ln1_gain).astype(jnp.bfloat16)
    whole = lax.all_gather(normed, "mp", axis=1, tiled=True)
    local_width = qkv_weight.shape[2]
    columns = whole
    projected = jnp.einsum(
        "ind,cdf->cinf",
        columns,
        lax.all_gather(qkv_weight, "dp", axis=1, tiled=True),
        preferred_element_type=jnp.float32,
    ).astype(jnp.bfloat16)
    local_heads = local_width // head_size
    shaped = projected.reshape(3, images, length, local_heads, head_size)
    queries = shaped[0]
    keys_all = shaped[1]
    values_all = shaped[2]
    size_bias = jnp.log(sizes)[:, None, None, :]
    block = min(512, length)
    outputs = []
    for begin in range(0, length, block):
        scores = (
            jnp.einsum(
                "iqhe,ikhe->ihqk",
                queries[:, begin : begin + block],
                keys_all,
                preferred_element_type=jnp.float32,
            )
            / math.sqrt(head_size)
            + size_bias
        )
        weights = jax.nn.softmax(scores, axis=-1).astype(jnp.bfloat16)
        attended_block = jnp.einsum(
            "ihqk,ikhe->iqhe", weights, values_all, preferred_element_type=jnp.float32
        )
        outputs.append(attended_block.astype(jnp.bfloat16).reshape(images, block, local_width))
    attended = jnp.concatenate(outputs, axis=1)
    branch = jnp.einsum(
        "ind,de->ine",
        attended,
        lax.all_gather(proj_weight, "dp", axis=1, tiled=True),
        preferred_element_type=jnp.float32,
    )
    weighted = sizes[:, :, None] * branch
    own_sizes = lax.dynamic_slice_in_dim(sizes, own_start, own_tokens, 1)
    own_weighted = own_sizes[:, :, None] * base
    local_total = lax.dynamic_update_slice_in_dim(
        weighted,
        lax.dynamic_slice_in_dim(weighted, own_start, own_tokens, 1) + own_weighted,
        own_start,
        1,
    )
    merged_count = kept_total // devices_mp
    own_order = lax.dynamic_slice_in_dim(
        kept_order, lax.axis_index("mp") * merged_count, merged_count, 1
    )
    scattered = lax.psum_scatter(
        jnp.transpose(
            merge_rows(local_total, kept_order, pair_source, pair_target), (1, 0, 2)
        ).astype(jnp.bfloat16),
        "mp",
        scatter_dimension=0,
        tiled=True,
    ).astype(jnp.float32)
    numerator = jnp.transpose(scattered, (1, 0, 2))
    merged_size = merge_rows(sizes[:, :, None], own_order, pair_source, pair_target)
    merged = numerator / merged_size
    normed_two = layer_norm(merged, ln2_gain).astype(jnp.bfloat16)
    gathered = lax.all_gather(normed_two, "mp", axis=1, tiled=True)
    columns = gathered
    hidden_sum = jnp.einsum(
        "imd,df->imf",
        columns,
        lax.all_gather(fc1_weight, "dp", axis=0, tiled=True),
        preferred_element_type=jnp.float32,
    )
    hidden = jax.nn.gelu(hidden_sum + fc1_bias).astype(jnp.bfloat16)
    partial_out = jnp.einsum(
        "imf,fd->imd",
        hidden,
        lax.all_gather(fc2_weight, "dp", axis=1, tiled=True),
        preferred_element_type=jnp.float32,
    )
    mlp_part = lax.psum_scatter(
        partial_out.astype(jnp.bfloat16), "mp", scatter_dimension=1, tiled=True
    ).astype(jnp.float32)
    return (merged + mlp_part).astype(jnp.bfloat16)


def solution(mesh):
    return jax.shard_map(
        shards,
        mesh=mesh,
        in_specs=(
            P("dp", "mp", None),
            P("dp", None),
            P(),
            P(None, "dp", "mp"),
            P("mp", "dp"),
            P(),
            P("dp", "mp"),
            P("mp"),
            P("mp", "dp"),
            P("dp", None),
            P("dp", None),
            P("dp", None),
        ),
        out_specs=P("dp", "mp", None),
        check_vma=False,
    )
```

profile of v0, /device:TPU:1, one launch (start us, length us, event | category | flops | bytes accessed | tf_op | source)
XLA Modules:
  0.0 317.7 jit_solution(4380768634615341311)
XLA Ops:
  6.5 0.0 all-gather.6.cloned.1.call-start
  6.6 1.3 convert_reduce_fusion
  7.9 1.4 fusion.30
  9.3 2.2 fusion.32
  11.5 0.0 all-gather.6.cloned.1.call-update
  11.6 0.0 all-gather.8.cloned.1.call-start
  11.6 0.7 all-gather.8.cloned.1.call-update
  12.3 0.0 all-gather.12.cloned.1.call-start
  12.4 0.7 all-gather.12.cloned.1.call-update
  13.0 0.0 all-gather.14.cloned.1.call-start
  13.1 0.5 all-gather.14.cloned.1.call-update
  13.6 0.0 all-gather.10.cloned.1.call-start
  13.8 28.3 %all_gather.20 = bf16[320,1280]{0,1:T(8,128)(2,1)S(1)} all-gather(bf16[320,160]{0,1:T(8,128)(2,1)S(1)} %copy-done.2), channel_id=1, replica_groups=mesh['dp'=8,'mp'=4] {'dp'}, dimensions={1}, use_global_device_ids=true | all-gather | bytes 921600 | tf_op jit(solution)/shard_map/all_gather | solution.py:85
  42.1 0.1 compare_select_fusion.2
  42.2 0.6 gather_fusion.3
  42.8 1.4 gather_fusion.2
  44.2 0.2 fusion.56
  44.4 53.4 %all-gather.8.cloned.1.call-done = bf16[3,1280,320]{2,1,0:T(8,128)(2,1)} async-done(((bf16[3,160,320]{2,1,0:T(8,128)(2,1)}), bf16[3,1280,320]{2,1,0:T(8,128)(2,1)}) %all-gather.8.cloned.1.call-update) | async-done | bytes 2457616 | tf_op jit(solution)/shard_map/all_gather | solution.py:54
  97.8 5.4 %convert_bitcast_fusion = bf16[3,1,1024,320]{2,3,0,1:T(8,128)(2,1)S(1)} fusion(bf16[3,1280,320]{2,1,0:T(8,128)(2,1)} %all-gather.8.cloned.1.call-done, bf16[1,1024,1280]{2,1,0:T(8,128)(2,1)} %all-gather.6.cloned.1.call-done), kind=kOutput, calls=%fused_computation.38 | convolution fusion | flops 2517565440 | bytes 7045120 | tf_op jit(solution)/shard_map/ind,cdf->cinf/dot_general | solution.py:51
  103.2 0.2 fusion.78
  103.3 4.9 %fusion.80 = (f32[4,512]{1,0:T(4,128)S(1)}, f32[4,512,1024]{2,1,0:T(8,128)}) fusion(f32[1024]{0:T(1024)S(1)} %bitcast.179, bf16[1024,4,80]{0,2,1:T(8,128)(2,1)S(1)} %bitcast.170, bf16[1,1024,4,80]{1,3,2,0:T(8,128)(2,1)S(1)} %bitcast.168), kind=kOutput, calls=%fused_computation.120 | convolution fusion | flops 343933952 | bytes 9383936 | tf_op jit(solution)/shard_map/sub | solution.py:76
  108.2 4.9 %fusion.79 = (f32[4,512]{1,0:T(4,128)S(1)}, f32[4,512,1024]{2,1,0:T(8,128)}) fusion(f32[1024]{0:T(1024)S(1)} %bitcast.180, bf16[1024,4,80]{0,2,1:T(8,128)(2,1)S(1)} %bitcast.171, bf16[1,1024,4,80]{1,3,2,0:T(8,128)(2,1)S(1)} %bitcast.169), kind=kOutput, calls=%fused_computation.119 | convolution fusion | flops 343933952 | bytes 9383936 | tf_op jit(solution)/shard_map/sub | solution.py:76
  113.0 5.1 %fusion.37 = bf16[4,80,512]{2,1,0:T(8,128)(2,1)S(1)} fusion(bf16[1024,4,80]{0,2,1:T(8,128)(2,1)S(1)} %bitcast.166, f32[4,512,1024]{2,1,0:T(8,128)} %get-tuple-element.13, f32[4,512]{1,0:T(4,128)S(1)} %get-tuple-element.12), kind=kOutput, calls=%fused_computation.55 | convolution fusion | flops 339902464 | bytes 9379840 | tf_op jit(solution)/shard_map/ihqk,ikhe->iqhe/dot_general | solution.py:77
  118.1 0.8 copy-done.9
  118.9 1.7 fusion.36
  120.6 4.0 %convolution_multiply_fusion = f32[1024,1280]{1,0:T(8,128)} fusion(bf16[320,1280]{0,1:T(8,128)(2,1)S(1)} %all_gather.20, f32[1024]{0:T(1024)S(1)} %bitcast.165, bf16[1,512,320]{1,2,0:T(8,128)(2,1)S(1)} %bitcast.173, bf16[1,512,320]{1,2,0:T(8,128)(2,1)S(1)} %bitcast.172), kind=kOutput, calls=%fused_computation.24 | convolution fusion | flops 841482240 | bytes 6721536 | tf_op jit(solution)/shard_map/ind,de->ine/dot_general | solution.py:82
  124.6 1.4 constant_dynamic-slice_fusion.2
  126.0 1.3 fusion.35
  127.3 3.1 gather_fusion.1
  130.5 9.7 %gather_fusion = f32[1008,1280]{1,0:T(8,128)} fusion(f32[1024,1280]{1,0:T(8,128)} %fusion.35, s32[1024]{0:T(1024)S(1)} %pad_clamp_fusion.2), kind=kCustom, calls=%fused_computation | custom fusion | bytes 10325952 | tf_op jit(solution)/shard_map/jit(take_along_axis)/gather | solution.py:18
  140.1 5.1 %fusion.21 = bf16[1008,1,1280]{2,0,1:T(8,128)(2,1)S(1)} fusion(f32[1008,1280]{1,0:T(8,128)} %gather_fusion, pred[1008]{0:T(1024)(128)(4,1)S(1)} %compare_and_fusion, f32[16,1280]{1,0:T(8,128)S(1)} %gather_fusion.1, pred[16]{0:T(512)(128)(4,1)S(1)} %compare_and_fusion.1, s32[1008]{0:T(1024)S(1)} %bitcast.175, s32[16]{0:T(128)S(1)} %bitcast.185), kind=kOutput, calls=%fused_computation.33 | convolution fusion | flops 251633408 | bytes 7828480 | tf_op jit(solution)/shard_map/icr,ird->icd/dot_general | solution.py:21
  145.2 27.6 %fusion = bf16[256,1280]{1,0:T(8,128)(2,1)S(1)} fusion(bf16[1008,1,1280]{2,0,1:T(8,128)(2,1)S(1)} %fusion.21), kind=kCustom, calls=%all-reduce-scatter | all-reduce-scatter fusion | flops 1310721 | bytes 3236352
  172.8 4.4 %collective-permute-start = (bf16[12,1280]{1,0:T(8,128)(2,1)S(1)}, bf16[12,1280]{1,0:T(8,128)(2,1)S(1)}, u32[]{:S(2)}, u32[]{:S(2)}) collective-permute-start(bf16[12,1280]{1,0:T(8,128)(2,1)S(1)} %slice.36), channel_id=1, source_target_pairs={{0,1},{1,2},{2,3},{4,5},{5,6},{6,7},{8,9},{9,10},{10,11},{12,13},{... | collective-permute-start | bytes 92168
  177.2 0.6 dynamic-slice.10
  178.5 1.1 concatenate.4
  179.6 0.4 fusion.46
  180.0 0.5 multiply_reduce_fusion
  180.5 0.4 multiply_convert_fusion
  180.9 2.1 copy.14
  183.0 0.0 all-gather.12.cloned.1.call-done
  183.1 39.2 %all-gather.14.cloned.1.call-done = bf16[1280,1280]{0,1:T(8,128)(2,1)} async-done(((bf16[1280,160]{0,1:T(8,128)(2,1)}), bf16[1280,1280]{0,1:T(8,128)(2,1)}) %all-gather.14.cloned.1.call-update) | async-done | bytes 3276816 | tf_op jit(solution)/shard_map/all_gather | solution.py:125
  222.2 42.2 %all-gather.10.cloned.1.call-done = bf16[1,1008,1280]{2,0,1:T(2,128)(2,1)} async-done(((bf16[1,252,1280]{2,0,1:T(2,128)(2,1)}), bf16[1,1008,1280]{2,0,1:T(2,128)(2,1)}) %all-gather.10.cloned.1.call-update) | async-done | bytes 2580496 | tf_op jit(solution)/shard_map/all_gather | solution.py:113
  264.5 12.8 %fusion.20 = bf16[1,1008,1280]{2,1,0:T(8,128)(2,1)} fusion(bf16[1280,1280]{0,1:T(8,128)(2,1)} %all-gather.14.cloned.1.call-done, bf16[1280,1280]{1,0:T(8,128)(2,1)} %all-gather.12.cloned.1.call-done, bf16[1,1008,1280]{2,0,1:T(2,128)(2,1)} %all-gather.10.cloned.1.call-done, f32[1280]{0:T(1024)S(1)} %copy-done.7), kind=kOutput, calls=%fused_computation.32 | convolution fusion | flops 6620221440 | bytes 11719680 | tf_op jit(solution)/shard_map/imf,fd->imd/dot_general | solution.py:122
  277.3 26.0 %fusion.1 = bf16[256,1280]{1,0:T(8,128)(2,1)S(1)} fusion(bf16[1,1008,1280]{2,1,0:T(8,128)(2,1)} %fusion.20), kind=kCustom, calls=%all-reduce-scatter.1 | all-reduce-scatter fusion | flops 1310721 | bytes 3236352
  303.4 4.4 %collective-permute-start.1 = (bf16[12,1280]{1,0:T(8,128)(2,1)S(1)}, bf16[12,1280]{1,0:T(8,128)(2,1)S(1)}, u32[]{:S(2)}, u32[]{:S(2)}) collective-permute-start(bf16[12,1280]{1,0:T(8,128)(2,1)S(1)} %slice.37), channel_id=1, source_target_pairs={{0,1},{1,2},{2,3},{4,5},{5,6},{6,7},{8,9},{9,10},{10,11},{12,13},{... | collective-permute-start | bytes 92168
  307.8 1.1 collective-permute-done.1
  308.9 1.0 concatenate.5
  309.9 1.3 add_convert_fusion.1
  (38 shorter events, 0.2 us)
Async XLA Ops:
  6.5 7.1 %copy-start.8 = (s32[1,16]{1,0:T(1,128)S(1)}, s32[1,16]{1,0:T(1,128)}, u32[]{:S(2)}) copy-start(s32[1,16]{1,0:T(1,128)} %param.21) | copy-start | bytes 196
  6.5 7.2 %copy-start = (f32[1,1024]{1,0:T(1,128)S(1)}, f32[1,1024]{1,0:T(1,128)}, u32[]{:S(2)}) copy-start(f32[1,1024]{1,0:T(1,128)} %param.13) | copy-start | bytes 12292
  6.5 7.2 %copy-start.2 = (bf16[320,160]{0,1:T(8,128)(2,1)S(1)}, bf16[320,160]{0,1:T(8,128)(2,1)}, u32[]{:S(2)}) copy-start(bf16[320,160]{0,1:T(8,128)(2,1)} %param.16) | copy-start | bytes 307204
  6.5 35.5 %copy-start.3 = (s32[1,1008]{1,0:T(1,128)S(1)}, s32[1,1008]{1,0:T(1,128)}, u32[]{:S(2)}) copy-start(s32[1,1008]{1,0:T(1,128)} %param.23) | copy-start | bytes 12100
  6.5 37.8 %all-gather.6.cloned.1.call-start = ((), (), s32[]{:S(2)}) async-start(), calls=%async_computation | async-start | bytes 3276800 | tf_op jit(solution)/shard_map/all_gather | solution.py:48
  7.9 36.3 %copy-start.5 = (s32[1,16]{1,0:T(1,128)S(1)}, s32[1,16]{1,0:T(1,128)}, u32[]{:S(2)}) copy-start(s32[1,16]{1,0:T(1,128)} %param.22) | copy-start | bytes 196
  11.6 86.2 %all-gather.8.cloned.1.call-start = ((), (), s32[]{:S(2)}) async-start(), calls=%async_computation.1 | async-start | bytes 3317760 | tf_op jit(solution)/shard_map/all_gather | solution.py:54
  12.3 170.7 %all-gather.12.cloned.1.call-start = ((), (), s32[]{:S(2)}) async-start(), calls=%async_computation.3 | async-start | bytes 3686400 | tf_op jit(solution)/shard_map/all_gather | solution.py:118
  13.0 209.2 %all-gather.14.cloned.1.call-start = ((), (), s32[]{:S(2)}) async-start(), calls=%async_computation.4 | async-start | bytes 3686400 | tf_op jit(solution)/shard_map/all_gather | solution.py:125
  13.6 250.8 %all-gather.10.cloned.1.call-start = ((), (), s32[]{:S(2)}) async-start(), calls=%async_computation.2 | async-start | bytes 6451200 | tf_op jit(solution)/shard_map/all_gather | solution.py:113
  113.0 5.9 %copy-start.9 = (f32[4,512,1024]{2,1,0:T(8,128)S(1)}, f32[4,512,1024]{2,1,0:T(8,128)}, u32[]{:S(2)}) copy-start(f32[4,512,1024]{2,1,0:T(8,128)} %get-tuple-element.11) | copy-start | bytes 25165828
  120.6 5.4 %copy-start.1 = (bf16[1,256,1280]{2,1,0:T(8,128)(2,1)S(1)}, bf16[1,256,1280]{2,1,0:T(8,128)(2,1)}, u32[]{:S(2)}) copy-start(bf16[1,256,1280]{2,1,0:T(8,128)(2,1)} %param.12) | copy-start | bytes 1966084
  145.2 32.0 %copy-start.6 = (u32[32]{0:T(128)S(1)}, u32[32]{0:T(128)}, u32[]{:S(2)}) copy-start(u32[32]{0:T(128)} %constant.99) | copy-start | bytes 388
  145.2 35.3 %copy-start.4 = (f32[1280]{0:T(1024)S(1)}, f32[1280]{0:T(1024)}, u32[]{:S(2)}) copy-start(f32[1280]{0:T(1024)} %param.17) | copy-start | bytes 15364
  172.8 5.7 %collective-permute-start = (bf16[12,1280]{1,0:T(8,128)(2,1)S(1)}, bf16[12,1280]{1,0:T(8,128)(2,1)S(1)}, u32[]{:S(2)}, u32[]{:S(2)}) collective-permute-start(bf16[12,1280]{1,0:T(8,128)(2,1)S(1)} %slice.36), channel_id=1, source_target_pairs={{0,1},{1,2},{2,3},{4,5},{5,6},{6,7},{8,9},{9,10},{10,11},{12,13},{... | collective-permute-start | bytes 92168
  179.6 84.9 %copy-start.7 = (f32[1280]{0:T(1024)S(1)}, f32[1280]{0:T(1024)}, u32[]{:S(2)}) copy-start(f32[1280]{0:T(1024)} %param.19) | copy-start | bytes 15364
  303.4 5.5 %collective-permute-start.1 = (bf16[12,1280]{1,0:T(8,128)(2,1)S(1)}, bf16[12,1280]{1,0:T(8,128)(2,1)S(1)}, u32[]{:S(2)}, u32[]{:S(2)}) collective-permute-start(bf16[12,1280]{1,0:T(8,128)(2,1)S(1)} %slice.37), channel_id=1, source_target_pairs={{0,1},{1,2},{2,3},{4,5},{5,6},{6,7},{8,9},{9,10},{10,11},{12,13},{... | collective-permute-start | bytes 92168
Sparse Core Ops, SparseCore 0:
  11.7 27.9 all-gather.5
  41.9 55.8 all-gather.7
  100.0 59.9 all-gather.11
  162.0 60.1 all-gather.13
  223.6 40.7 all-gather.9
where the time goes:
time: 318 us
  waiting for transfers between devices  138 us (43%)
  blocking collectives  81.9 us (26%)
  matrix products  44 us (14%)
  local copies, waits for them, and re-layouts  22 us (7%)
  between operations  14.1 us (4%)
  starting transfers between devices  8.96 us (3%)
  other arithmetic  8.93 us (3%)
    unnamed x2, blocking collectives  53.6 us
    all_gather x1, waiting for transfers between devices, shards(): lax.all_gather(qkv_weight, 'dp', axis=1, tiled=True)  53.4 us
    all_gather x1, waiting for transfers between devices, shards(): gathered = lax.all_gather(normed_two, 'mp', axis=1, tiled=True)  42.2 us
    all_gather x1, waiting for transfers between devices, shards(): lax.all_gather(fc2_weight, 'dp', axis=1, tiled=True)  39.2 us
    all_gather x1, blocking collectives, shards(): lax.all_gather(proj_weight, 'dp', axis=1, tiled=True)  28.3 us
    dot_general x1, matrix products, shards(): jnp.einsum('imf,fd->imd', hidden, lax.all_gather(fc2_weight, 'dp', axis=1...  12.8 us
    gather x2, local copies, waits for them, and re-layouts, merge_rows(): kept_rows = jnp.take_along_axis(total, order_rows[:, :, None], axis=1)  11 us
    sub x2, matrix products, shards(): weights = jax.nn.softmax(scores, axis=-1).astype(jnp.bfloat16)  9.7 us
  transfers between devices with their start and end apart: 7, of which 4 were waited for; matrix products, arithmetic and copies ran while one was open for 26% of the time, Pallas kernels for 0%

commit v1 on v0

--- a/solution.py
+++ b/solution.py
@@ -1,3 +1,4 @@
+import functools
 import math
 import jax
 import jax.numpy as jnp
@@ -6,6 +7,22 @@
 
 D = 1280
 HEADS = 16
+
+
+def try_all_gates(incoming_x, a_name):
+    shares = lax.axis_size(a_name)
+    grid = [incoming_x]
+    for q in range(shares - 1):
+        z = lax.ppermute(
+            grid[-1], axis_name=a_name, perm=[(i, (i + 1) % shares) for i in range(shares)]
+        )
+        grid.append(z)
+    x_next = jnp.concatenate(grid[::-1], axis=1)
+    aux = lax.axis_index(a_name)
+    return jnp.roll(x_next, (aux + 1) * incoming_x.shape[1], axis=1)
+
+
+reach_the_samples = functools.partial(try_all_gates, a_name="mp")
 
 
 def layer_norm(values, gain):
@@ -110,7 +127,7 @@
     merged_size = merge_rows(sizes[:, :, None], own_order, pair_source, pair_target)
     merged = numerator / merged_size
     normed_two = layer_norm(merged, ln2_gain).astype(jnp.bfloat16)
-    gathered = lax.all_gather(normed_two, "mp", axis=1, tiled=True)
+    gathered = reach_the_samples(normed_two)
     columns = gathered
     hidden_sum = jnp.einsum(
         "imd,df->imf",

time: 318 us -> 288 us (0.906)
  waiting for transfers between devices: 138 us -> 79 us
  local copies, waits for them, and re-layouts: 22 us -> 42.8 us
  starting transfers between devices: 8.96 us -> 16 us
    all_gather x1 -> x0, waiting for transfers between devices: 42.2 us -> none  [shards(): gathered = lax.all_gather(normed_two, 'mp', axis=1, tiled=True)]
    all_gather x1, waiting for transfers between devices: 39.2 us -> 0.01 us  [shards(): lax.all_gather(fc2_weight, 'dp', axis=1, tiled=True)]
    concatenate x0 -> x1, local copies, waits for them, and re-layouts: none -> 22.8 us  [try_all_gates(): return jnp.roll(x_next, (aux + 1) * incoming_x.shape[1], axis=1)]
    ppermute x0 -> x3, waiting for transfers between devices: none -> 22.6 us  [try_all_gates(): lax.ppermute(grid[-1], axis_name=a_name, perm=[(i, (i + 1) % shares) for...]
    ppermute x0 -> x3, starting transfers between devices: none -> 7.1 us  [try_all_gates(): lax.ppermute(grid[-1], axis_name=a_name, perm=[(i, (i + 1) % shares) for...]
  transfers between devices with their start and end apart: 7 -> 9, of which waited for: 4 -> 5; matrix products, arithmetic and copies ran while one was open for 26% -> 36% of each run, Pallas kernels for 0% -> 0%
where the time goes in v1:
time: 288 us; the launch traced here: 287 us
  blocking collectives  82.6 us (29%)
  waiting for transfers between devices  79 us (27%)
  matrix products  43.6 us (15%)
  local copies, waits for them, and re-layouts  42.8 us (15%)
  starting transfers between devices  16 us (6%)
  between operations  14.1 us (5%)
  other arithmetic  8.93 us (3%)
    unnamed x2, blocking collectives  54.3 us
    all_gather x1, waiting for transfers between devices, shards(): lax.all_gather(qkv_weight, 'dp', axis=1, tiled=True)  53.4 us
    all_gather x1, blocking collectives, shards(): lax.all_gather(proj_weight, 'dp', axis=1, tiled=True)  28.3 us
    concatenate x1, local copies, waits for them, and re-layouts, try_all_gates(): return jnp.roll(x_next, (aux + 1) * incoming_x.shape[1], axis=1)  22.8 us
    ppermute x3, waiting for transfers between devices, try_all_gates(): lax.ppermute(grid[-1], axis_name=a_name, perm=[(i, (i + 1) % shares) for...  22.6 us
    dot_general x1, matrix products, shards(): jnp.einsum('imf,fd->imd', hidden, lax.all_gather(fc2_weight, 'dp', axis=1...  12.5 us
    gather x2, local copies, waits for them, and re-layouts, merge_rows(): kept_rows = jnp.take_along_axis(total, order_rows[:, :, None], axis=1)  11 us
    sub x2, matrix products, shards(): weights = jax.nn.softmax(scores, axis=-1).astype(jnp.bfloat16)  9.7 us
  transfers between devices with their start and end apart: 9, of which 5 were waited for; matrix products, arithmetic and copies ran while one was open for 36% of the time, Pallas kernels for 0%

profile of v1, /device:TPU:1, one launch (start us, length us, event | category | flops | bytes accessed | tf_op | source)
XLA Modules:
  0.0 287.0 jit_solution(2579341762247655634)
XLA Ops:
  6.6 1.3 convert_reduce_fusion
  7.9 1.4 fusion.30
  9.3 2.2 fusion.32
  11.6 0.0 all-gather.7.cloned.1.call-start
  11.6 0.7 all-gather.7.cloned.1.call-update
  12.3 0.0 all-gather.11.cloned.1.call-start
  12.4 0.7 all-gather.11.cloned.1.call-update
  13.0 0.0 all-gather.9.cloned.1.call-start
  13.1 0.5 all-gather.9.cloned.1.call-update
  13.7 28.3 %all_gather.17 = bf16[320,1280]{0,1:T(8,128)(2,1)S(1)} all-gather(bf16[320,160]{0,1:T(8,128)(2,1)S(1)} %copy-done.2), channel_id=1, replica_groups=mesh['dp'=8,'mp'=4] {'dp'}, dimensions={1}, use_global_device_ids=true | all-gather | bytes 921600 | tf_op jit(solution)/shard_map/all_gather | solution.py:102
  42.0 0.1 compare_select_fusion.2
  42.1 0.6 gather_fusion.3
  42.8 1.4 gather_fusion.2
  44.2 0.2 fusion.56
  44.3 53.4 %all-gather.7.cloned.1.call-done = bf16[3,1280,320]{2,1,0:T(8,128)(2,1)} async-done(((bf16[3,160,320]{2,1,0:T(8,128)(2,1)}), bf16[3,1280,320]{2,1,0:T(8,128)(2,1)}) %all-gather.7.cloned.1.call-update) | async-done | bytes 2457616 | tf_op jit(solution)/shard_map/all_gather | solution.py:71
  97.8 5.4 %convert_bitcast_fusion = bf16[3,1,1024,320]{2,3,0,1:T(8,128)(2,1)S(1)} fusion(bf16[3,1280,320]{2,1,0:T(8,128)(2,1)} %all-gather.7.cloned.1.call-done, bf16[1,1024,1280]{2,1,0:T(8,128)(2,1)} %all-gather.5.cloned.1.call-done), kind=kOutput, calls=%fused_computation.38 | convolution fusion | flops 2517565440 | bytes 7045120 | tf_op jit(solution)/shard_map/ind,cdf->cinf/dot_general | solution.py:68
  103.2 0.2 fusion.80
  103.3 4.9 %fusion.82 = (f32[4,512]{1,0:T(4,128)S(1)}, f32[4,512,1024]{2,1,0:T(8,128)}) fusion(f32[1024]{0:T(1024)S(1)} %bitcast.179, bf16[1024,4,80]{0,2,1:T(8,128)(2,1)S(1)} %bitcast.170, bf16[1,1024,4,80]{1,3,2,0:T(8,128)(2,1)S(1)} %bitcast.168), kind=kOutput, calls=%fused_computation.121 | convolution fusion | flops 343933952 | bytes 9383936 | tf_op jit(solution)/shard_map/sub | solution.py:93
  108.2 4.9 %fusion.81 = (f32[4,512]{1,0:T(4,128)S(1)}, f32[4,512,1024]{2,1,0:T(8,128)}) fusion(f32[1024]{0:T(1024)S(1)} %bitcast.180, bf16[1024,4,80]{0,2,1:T(8,128)(2,1)S(1)} %bitcast.171, bf16[1,1024,4,80]{1,3,2,0:T(8,128)(2,1)S(1)} %bitcast.169), kind=kOutput, calls=%fused_computation.120 | convolution fusion | flops 343933952 | bytes 9383936 | tf_op jit(solution)/shard_map/sub | solution.py:93
  113.0 5.1 %fusion.37 = bf16[4,80,512]{2,1,0:T(8,128)(2,1)S(1)} fusion(bf16[1024,4,80]{0,2,1:T(8,128)(2,1)S(1)} %bitcast.166, f32[4,512,1024]{2,1,0:T(8,128)} %get-tuple-element.13, f32[4,512]{1,0:T(4,128)S(1)} %get-tuple-element.12), kind=kOutput, calls=%fused_computation.55 | convolution fusion | flops 339902464 | bytes 9379840 | tf_op jit(solution)/shard_map/ihqk,ikhe->iqhe/dot_general | solution.py:94
  118.1 0.8 copy-done.9
  118.9 1.7 fusion.36
  120.6 4.0 %convolution_multiply_fusion = f32[1024,1280]{1,0:T(8,128)} fusion(bf16[320,1280]{0,1:T(8,128)(2,1)S(1)} %all_gather.17, f32[1024]{0:T(1024)S(1)} %bitcast.165, bf16[1,512,320]{1,2,0:T(8,128)(2,1)S(1)} %bitcast.173, bf16[1,512,320]{1,2,0:T(8,128)(2,1)S(1)} %bitcast.172), kind=kOutput, calls=%fused_computation.24 | convolution fusion | flops 841482240 | bytes 6721536 | tf_op jit(solution)/shard_map/ind,de->ine/dot_general | solution.py:99
  124.6 1.4 constant_dynamic-slice_fusion.2
  126.0 1.3 fusion.35
  127.3 3.1 %gather_fusion.1 = f32[16,1280]{1,0:T(8,128)S(1)} fusion(f32[1024,1280]{1,0:T(8,128)} %fusion.35, s32[1024]{0:T(1024)S(1)} %pad_clamp_fusion.1), kind=kCustom, calls=%fused_computation.1 | custom fusion | bytes 163904 | tf_op jit(solution)/shard_map/jit(take_along_axis)/gather | solution.py:36
  130.5 9.7 %gather_fusion = f32[1008,1280]{1,0:T(8,128)} fusion(f32[1024,1280]{1,0:T(8,128)} %fusion.35, s32[1024]{0:T(1024)S(1)} %pad_clamp_fusion.2), kind=kCustom, calls=%fused_computation | custom fusion | bytes 10325952 | tf_op jit(solution)/shard_map/jit(take_along_axis)/gather | solution.py:35
  140.1 5.1 %fusion.21 = bf16[1008,1,1280]{2,0,1:T(8,128)(2,1)S(1)} fusion(f32[1008,1280]{1,0:T(8,128)} %gather_fusion, pred[1008]{0:T(1024)(128)(4,1)S(1)} %compare_and_fusion, f32[16,1280]{1,0:T(8,128)S(1)} %gather_fusion.1, pred[16]{0:T(512)(128)(4,1)S(1)} %compare_and_fusion.1, s32[1008]{0:T(1024)S(1)} %bitcast.175, s32[16]{0:T(128)S(1)} %bitcast.185), kind=kOutput, calls=%fused_computation.33 | convolution fusion | flops 251633408 | bytes 7828480 | tf_op jit(solution)/shard_map/icr,ird->icd/dot_general | solution.py:38
  145.2 27.6 %fusion = bf16[256,1280]{1,0:T(8,128)(2,1)S(1)} fusion(bf16[1008,1,1280]{2,0,1:T(8,128)(2,1)S(1)} %fusion.21), kind=kCustom, calls=%all-reduce-scatter | all-reduce-scatter fusion | flops 1310721 | bytes 3236352
  172.8 4.4 %collective-permute-start.3 = (bf16[12,1280]{1,0:T(8,128)(2,1)S(1)}, bf16[12,1280]{1,0:T(8,128)(2,1)S(1)}, u32[]{:S(2)}, u32[]{:S(2)}) collective-permute-start(bf16[12,1280]{1,0:T(8,128)(2,1)S(1)} %slice.36), channel_id=1, source_target_pairs={{0,1},{1,2},{2,3},{4,5},{5,6},{6,7},{8,9},{9,10},{10,11},{12,13},{... | collective-permute-start | bytes 92168
  177.2 0.6 dynamic-slice.10
  178.5 1.1 concatenate.11
  179.6 0.4 fusion.46
  180.0 0.5 multiply_reduce_fusion
  180.5 0.4 multiply_convert_fusion
  180.9 2.1 collective-permute-start
  183.0 7.5 %collective-permute-done = bf16[1,252,1280]{2,1,0:T(8,128)(2,1)S(1)} collective-permute-done((bf16[1,252,1280]{2,1,0:T(8,128)(2,1)S(1)}, bf16[1,252,1280]{2,1,0:T(8,128)(2,1)S(1)}, u32[]{:S(2)}, u32[]{:S(2)}) %collective-permute-start) | collective-permute-done | bytes 645152 | tf_op jit(solution)/shard_map/ppermute | solution.py:16
  190.6 2.5 collective-permute-start.1
  193.1 7.5 %collective-permute-done.1 = bf16[1,252,1280]{2,1,0:T(8,128)(2,1)S(1)} collective-permute-done((bf16[1,252,1280]{2,1,0:T(8,128)(2,1)S(1)}, bf16[1,252,1280]{2,1,0:T(8,128)(2,1)S(1)}, u32[]{:S(2)}, u32[]{:S(2)}) %collective-permute-start.1) | collective-permute-done | bytes 645152 | tf_op jit(solution)/shard_map/ppermute | solution.py:16
  200.6 2.5 collective-permute-start.2
  203.1 7.5 %collective-permute-done.2 = bf16[1,252,1280]{2,1,0:T(8,128)(2,1)S(1)} collective-permute-done((bf16[1,252,1280]{2,1,0:T(8,128)(2,1)S(1)}, bf16[1,252,1280]{2,1,0:T(8,128)(2,1)S(1)}, u32[]{:S(2)}, u32[]{:S(2)}) %collective-permute-start.2) | collective-permute-done | bytes 645152 | tf_op jit(solution)/shard_map/ppermute | solution.py:16
  210.6 22.8 %concatenate.10 = bf16[1,2016,1280]{2,1,0:T(8,128)(2,1)} concatenate(bf16[1,252,1280]{2,1,0:T(8,128)(2,1)S(1)} %collective-permute-done.2, bf16[1,252,1280]{2,1,0:T(8,128)(2,1)S(1)} %collective-permute-done.1, bf16[1,252,1280]{2,1,0:T(8,128)(2,1)S(1)} %collective-permute-done, bf16[1,252,1280]{2,1,0:T(8,128)(2,1)S(1)} %multiply_convert_fusion, ...), dimensions={1} | concatenate | bytes 10321920 | tf_op jit(solution)/shard_map/jit(_roll_dynamic)/concatenate | solution.py:22
  233.5 12.5 %fusion.20 = bf16[1,1008,1280]{2,1,0:T(8,128)(2,1)} fusion(bf16[1280,1280]{0,1:T(8,128)(2,1)} %all-gather.11.cloned.1.call-done, bf16[1280,1280]{1,0:T(8,128)(2,1)} %all-gather.9.cloned.1.call-done, f32[1280]{0:T(1024)S(1)} %copy-done.7, bf16[1,2016,1280]{2,1,0:T(8,128)(2,1)} %concatenate.10, s32[]{:T(128)S(6)} %select_n.178), kind=kOutput, calls=%fused_computation.32 | convolution fusion | flops 6620221440 | bytes 11719684 | tf_op jit(solution)/shard_map/imf,fd->imd/dot_general | solution.py:139
  246.0 26.7 %fusion.1 = bf16[256,1280]{1,0:T(8,128)(2,1)S(1)} fusion(bf16[1,1008,1280]{2,1,0:T(8,128)(2,1)} %fusion.20), kind=kCustom, calls=%all-reduce-scatter.1 | all-reduce-scatter fusion | flops 1310721 | bytes 3236352
  272.7 4.4 %collective-permute-start.4 = (bf16[12,1280]{1,0:T(8,128)(2,1)S(1)}, bf16[12,1280]{1,0:T(8,128)(2,1)S(1)}, u32[]{:S(2)}, u32[]{:S(2)}) collective-permute-start(bf16[12,1280]{1,0:T(8,128)(2,1)S(1)} %slice.37), channel_id=1, source_target_pairs={{0,1},{1,2},{2,3},{4,5},{5,6},{6,7},{8,9},{9,10},{10,11},{12,13},{... | collective-permute-start | bytes 92168
  277.1 1.1 collective-permute-done.4
  278.2 1.0 concatenate.12
  279.3 1.3 add_convert_fusion.1
  (41 shorter events, 0.2 us)
Async XLA Ops:
  6.5 7.1 %copy-start.8 = (s32[1,16]{1,0:T(1,128)S(1)}, s32[1,16]{1,0:T(1,128)}, u32[]{:S(2)}) copy-start(s32[1,16]{1,0:T(1,128)} %param.21) | copy-start | bytes 196
  6.5 7.1 %copy-start = (f32[1,1024]{1,0:T(1,128)S(1)}, f32[1,1024]{1,0:T(1,128)}, u32[]{:S(2)}) copy-start(f32[1,1024]{1,0:T(1,128)} %param.13) | copy-start | bytes 12292
  6.5 7.2 %copy-start.2 = (bf16[320,160]{0,1:T(8,128)(2,1)S(1)}, bf16[320,160]{0,1:T(8,128)(2,1)}, u32[]{:S(2)}) copy-start(bf16[320,160]{0,1:T(8,128)(2,1)} %param.16) | copy-start | bytes 307204
  6.5 35.4 %copy-start.3 = (s32[1,1008]{1,0:T(1,128)S(1)}, s32[1,1008]{1,0:T(1,128)}, u32[]{:S(2)}) copy-start(s32[1,1008]{1,0:T(1,128)} %param.23) | copy-start | bytes 12100
  6.5 37.8 %all-gather.5.cloned.1.call-start = ((), (), s32[]{:S(2)}) async-start(), calls=%async_computation | async-start | bytes 3276800 | tf_op jit(solution)/shard_map/all_gather | solution.py:65
  7.9 36.2 %copy-start.5 = (s32[1,16]{1,0:T(1,128)S(1)}, s32[1,16]{1,0:T(1,128)}, u32[]{:S(2)}) copy-start(s32[1,16]{1,0:T(1,128)} %param.22) | copy-start | bytes 196
  11.6 86.2 %all-gather.7.cloned.1.call-start = ((), (), s32[]{:S(2)}) async-start(), calls=%async_computation.1 | async-start | bytes 3317760 | tf_op jit(solution)/shard_map/all_gather | solution.py:71
  12.3 221.1 %all-gather.11.cloned.1.call-start = ((), (), s32[]{:S(2)}) async-start(), calls=%async_computation.3 | async-start | bytes 3686400 | tf_op jit(solution)/shard_map/all_gather | solution.py:142
  13.0 220.4 %all-gather.9.cloned.1.call-start = ((), (), s32[]{:S(2)}) async-start(), calls=%async_computation.2 | async-start | bytes 3686400 | tf_op jit(solution)/shard_map/all_gather | solution.py:135
  113.0 5.9 %copy-start.9 = (f32[4,512,1024]{2,1,0:T(8,128)S(1)}, f32[4,512,1024]{2,1,0:T(8,128)}, u32[]{:S(2)}) copy-start(f32[4,512,1024]{2,1,0:T(8,128)} %get-tuple-element.11) | copy-start | bytes 25165828
  120.6 5.4 %copy-start.1 = (bf16[1,256,1280]{2,1,0:T(8,128)(2,1)S(1)}, bf16[1,256,1280]{2,1,0:T(8,128)(2,1)}, u32[]{:S(2)}) copy-start(bf16[1,256,1280]{2,1,0:T(8,128)(2,1)} %param.12) | copy-start | bytes 1966084
  145.2 32.0 %copy-start.6 = (u32[32]{0:T(128)S(1)}, u32[32]{0:T(128)}, u32[]{:S(2)}) copy-start(u32[32]{0:T(128)} %constant.118) | copy-start | bytes 388
  145.2 35.3 %copy-start.4 = (f32[1280]{0:T(1024)S(1)}, f32[1280]{0:T(1024)}, u32[]{:S(2)}) copy-start(f32[1280]{0:T(1024)} %param.17) | copy-start | bytes 15364
  172.8 5.7 %collective-permute-start.3 = (bf16[12,1280]{1,0:T(8,128)(2,1)S(1)}, bf16[12,1280]{1,0:T(8,128)(2,1)S(1)}, u32[]{:S(2)}, u32[]{:S(2)}) collective-permute-start(bf16[12,1280]{1,0:T(8,128)(2,1)S(1)} %slice.36), channel_id=1, source_target_pairs={{0,1},{1,2},{2,3},{4,5},{5,6},{6,7},{8,9},{9,10},{10,11},{12,13},{... | collective-permute-start | bytes 92168
  180.9 9.7 %collective-permute-start = (bf16[1,252,1280]{2,1,0:T(8,128)(2,1)S(1)}, bf16[1,252,1280]{2,1,0:T(8,128)(2,1)S(1)}, u32[]{:S(2)}, u32[]{:S(2)}) collective-permute-start(bf16[1,252,1280]{2,1,0:T(8,128)(2,1)S(1)} %multiply_convert_fusion), channel_id=1, source_target_pairs={{0,1},{1,2},{2,3},{3,0},{4,5},{5,6},{6,7},{7,4},{8,9},{9,10},{10,1... | collective-permute-start | bytes 1935368 | tf_op jit(solution)/shard_map/ppermute | solution.py:16
  190.6 10.0 %collective-permute-start.1 = (bf16[1,252,1280]{2,1,0:T(8,128)(2,1)S(1)}, bf16[1,252,1280]{2,1,0:T(8,128)(2,1)S(1)}, u32[]{:S(2)}, u32[]{:S(2)}) collective-permute-start(bf16[1,252,1280]{2,1,0:T(8,128)(2,1)S(1)} %collective-permute-done), channel_id=1, source_target_pairs={{0,1},{1,2},{2,3},{3,0},{4,5},{5,6},{6,7},{7,4},{8,9},{9,10},{10,1... | collective-permute-start | bytes 1935368 | tf_op jit(solution)/shard_map/ppermute | solution.py:16
  200.6 10.0 %collective-permute-start.2 = (bf16[1,252,1280]{2,1,0:T(8,128)(2,1)S(1)}, bf16[1,252,1280]{2,1,0:T(8,128)(2,1)S(1)}, u32[]{:S(2)}, u32[]{:S(2)}) collective-permute-start(bf16[1,252,1280]{2,1,0:T(8,128)(2,1)S(1)} %collective-permute-done.1), channel_id=1, source_target_pairs={{0,1},{1,2},{2,3},{3,0},{4,5},{5,6},{6,7},{7,4},{8,9},{9,10},{10,1... | collective-permute-start | bytes 1935368 | tf_op jit(solution)/shard_map/ppermute | solution.py:16
  203.1 30.4 %copy-start.7 = (f32[1280]{0:T(1024)S(1)}, f32[1280]{0:T(1024)}, u32[]{:S(2)}) copy-start(f32[1280]{0:T(1024)} %param.19) | copy-start | bytes 15364
  272.7 5.5 %collective-permute-start.4 = (bf16[12,1280]{1,0:T(8,128)(2,1)S(1)}, bf16[12,1280]{1,0:T(8,128)(2,1)S(1)}, u32[]{:S(2)}, u32[]{:S(2)}) collective-permute-start(bf16[12,1280]{1,0:T(8,128)(2,1)S(1)} %slice.37), channel_id=1, source_target_pairs={{0,1},{1,2},{2,3},{4,5},{5,6},{6,7},{8,9},{9,10},{10,11},{12,13},{... | collective-permute-start | bytes 92168
Sparse Core Ops, SparseCore 0:
  11.7 27.9 all-gather.4
  41.9 55.8 all-gather.6
  100.0 59.9 all-gather.10
  162.0 60.1 all-gather.8
